TPU v7x, 32 devices: a whole 2x2x4 slice. The times are simulated.
32 devices in a mesh: pipe: 4 (over y, core), vocab: 2 (over x), expert: 4 (over z).
Axes of the slice: x: 2, y: 2, z: 4, core: 2. Of those that a mesh axis runs over, the one named last changes fastest.
Arguments:
- token_ids: int32 [192], replicated, may hold values from 0 to 65535
- routes: int32 [192, 2], replicated, may hold values from 0 to 3, all different within a row; in each aligned block of 192 rows (0 to 191, 192 to 383, ...) at most 144 rows name the same one
- gate_weights: float32 [192, 2], replicated, may hold values from 0.2 to 1
- embed_table: bfloat16 [65536, 7168], P(('pipe', 'vocab'), 'expert'), may hold values from -0.59765625 to 0.59765625
- w_gate: bfloat16 [4, 7168, 2048], P('expert', None, ('pipe', 'vocab')), may hold values from -0.5 to 0.5
- w_up: bfloat16 [4, 7168, 2048], P('expert', None, ('pipe', 'vocab')), may hold values from -0.5 to 0.5
- w_down: bfloat16 [4, 2048, 7168], P('expert', ('pipe', 'vocab')), may hold values from -0.125 to 0.125
Outputs:
- logits: bfloat16 [192, 65536], P('expert', ('pipe', 'vocab'))
Inputs may be any that keep to these rules, and one draw needn't show every extreme that they name: `routes`: each row names 2 different experts; over all 192 rows no expert is named more than 144 times, a bound that some block reaches.
All inputs are finite; a program needn't handle non-finite values.
Results may differ from a plain program's by a relative error of at most 0.025.
Values may be sent and summed in bfloat16 or wider, within the bound.
A program may use at most 128 MiB of HBM per device.

v0:
```python
import jax
import jax.numpy as jnp
from jax import lax
from jax.sharding import PartitionSpec as P


def per_device(token_ids, routes, gate_weights, embed_table, w_gate, w_up, w_down):
    vocab_rows, width_cols = embed_table.shape
    tokens, top_count = routes.shape
    experts = lax.axis_size("expert")
    group_size = lax.axis_size(("pipe", "vocab"))
    capacity = group_size * (3 * tokens * top_count // (2 * experts * group_size))
    row_base = lax.axis_index(("pipe", "vocab")) * vocab_rows
    local_ids = token_ids - row_base
    in_shard = (local_ids >= 0) & (local_ids < vocab_rows)
    lookup_rows = jnp.take(embed_table, jnp.clip(local_ids, 0, vocab_rows - 1), axis=0)
    lookup_rows = jnp.where(in_shard[:, None], lookup_rows.astype(jnp.float32), 0.0)
    embedded = lax.psum(lookup_rows.astype(jnp.bfloat16), ("pipe", "vocab"))
    flat_routes = routes.reshape(-1)
    one_hot = (flat_routes[:, None] == jnp.arange(experts, dtype=jnp.int32)[None, :]).astype(
        jnp.int32
    )
    slot_index = jnp.sum((jnp.cumsum(one_hot, axis=0) - one_hot) * one_hot, axis=1)
    slot_dest = flat_routes * capacity + slot_index
    repeated = jnp.repeat(embedded, top_count, axis=0)
    buffer = jnp.zeros((experts * capacity, width_cols), jnp.bfloat16).at[slot_dest].set(repeated)
    buffer = buffer.reshape(experts, capacity, width_cols)
    flat_rows = lax.all_to_all(buffer, "expert", split_axis=0, concat_axis=2, tiled=True)[0]
    gate_proj = jnp.dot(flat_rows, w_gate[0], preferred_element_type=jnp.float32)
    up_proj = jnp.dot(flat_rows, w_up[0], preferred_element_type=jnp.float32)
    hidden = (jax.nn.silu(gate_proj) * up_proj).astype(jnp.bfloat16)
    partial_value = jnp.dot(hidden, w_down[0], preferred_element_type=jnp.float32)[None]
    shared = lax.psum_scatter(
        partial_value.astype(jnp.bfloat16), ("pipe", "vocab"), scatter_dimension=1, tiled=True
    ).astype(jnp.float32)
    shared = lax.all_to_all(
        shared.astype(jnp.bfloat16), "expert", split_axis=2, concat_axis=0, tiled=True
    ).astype(shared.dtype)
    returned = lax.all_gather(
        shared.astype(jnp.bfloat16), ("pipe", "vocab"), axis=1, tiled=True
    ).astype(shared.dtype)
    picked = returned.reshape(experts * capacity, width_cols)[slot_dest].reshape(
        tokens, top_count, width_cols
    )
    moe_out = jnp.sum(picked * gate_weights[:, :, None], axis=1)
    residual = (embedded.astype(jnp.float32) + moe_out).astype(jnp.bfloat16)
    return lax.psum_scatter(
        lax.dot_general(
            residual, embed_table, (((1,), (1,)), ((), ())), preferred_element_type=jnp.float32
        ).astype(jnp.bfloat16),
        "expert",
        scatter_dimension=0,
        tiled=True,
    )


def solution(mesh):
    return jax.shard_map(
        per_device,
        mesh=mesh,
        in_specs=(
            P(),
            P(),
            P(),
            P(("pipe", "vocab"), "expert"),
            P("expert", None, ("pipe", "vocab")),
            P("expert", None, ("pipe", "vocab")),
            P("expert", ("pipe", "vocab"), None),
        ),
        out_specs=P("expert", ("pipe", "vocab")),
        check_vma=False,
    )
```

profile of v0, /device:TPU:0, one launch (start us, length us, event | category | flops | bytes accessed | tf_op | source)
XLA Modules:
  0.0 428.2 jit_solution(8567750402209135640)
XLA Ops:
  6.5 0.7 compare_and_fusion
  7.2 14.9 %gather_fusion = bf16[192,1792]{1,0:T(8,128)(2,1)S(1)} fusion(bf16[8192,1792]{1,0:T(8,128)(2,1)} %param.10, s32[1024]{0:T(1024)S(1)} %pad_clamp_fusion.1), kind=kCustom, calls=%fused_computation | custom fusion | bytes 1377024 | tf_op jit(solution)/shard_map/jit(_take)/gather | solution.py:16
  22.1 1.2 select_convert_fusion
  23.4 0.1 copy.39
  23.5 0.1 eq.29
  23.7 0.1 eq.25
  23.8 1.2 reduce-window.6
  25.1 0.2 slice_reduce_fusion
  25.3 0.2 reduce-window.9
  25.5 0.1 copy.38
  25.6 0.1 mul.44
  25.7 0.1 add_bitcast_fusion
  25.9 55.8 %all-reduce.4.cloned.1.call-done = bf16[192,1792]{1,0:T(8,128)(2,1)} async-done(((bf16[192,1792]{1,0:T(8,128)(2,1)}), bf16[192,1792]{1,0:T(8,128)(2,1)}) %all-reduce.4.cloned.1.call-update) | async-done | bytes 688144 | tf_op jit(solution)/shard_map/psum | solution.py:18
  81.6 1.8 broadcast_in_dim.42
  83.4 0.6 reshape.98
  84.0 3.3 scatter_custom_fusion
  87.3 51.2 %all_to_all.33 = bf16[4,144,1792]{2,1,0:T(8,128)(2,1)S(1)} all-to-all(bf16[4,144,1792]{2,1,0:T(8,128)(2,1)S(1)} %bitcast.66), channel_id=1, replica_groups=mesh['pipe'=4,'vocab'=2,'expert'=4] {'expert'}, dimensions={0} | all-to-all | bytes 4128768 | tf_op jit(solution)/shard_map/all_to_all | solution.py:28
  138.5 1.1 copy.41
  139.6 0.3 copy.50
  139.8 1.8 copy-done
  141.6 0.8 fusion.5
  142.4 6.9 %fusion.1 = bf16[1,144,7168]{2,1,0:T(8,128)(2,1)} fusion(bf16[1,256,7168]{2,1,0:T(8,128)(2,1)} %param.13, bf16[144,7168]{1,0:T(8,128)(2,1)S(1)} %bitcast.63, bf16[1,7168,256]{2,1,0:T(8,128)(2,1)} %param.12, f32[144,256]{1,0:T(8,128)S(1)} %fusion.5), kind=kOutput, calls=%fused_computation.5 | convolution fusion | flops 1058217984 | bytes 11616256 | tf_op jit(solution)/shard_map/dot_general | solution.py:32
  149.2 58.3 %fusion = bf16[24,7168]{1,0:T(8,128)(2,1)S(1)} fusion(bf16[1,144,7168]{2,1,0:T(8,128)(2,1)} %fusion.1), kind=kCustom, calls=%all-reduce-scatter | all-reduce-scatter fusion | flops 1376257 | bytes 2408960
  207.6 1.9 collective-permute-start
  209.5 0.1 slice.13
  209.6 1.7 collective-permute-start.1
  211.3 0.6 dynamic-slice.4
  212.6 4.5 %collective-permute-done = bf16[24,7168]{1,0:T(8,128)(2,1)S(1)} collective-permute-done((bf16[24,7168]{1,0:T(8,128)(2,1)S(1)}, bf16[24,7168]{1,0:T(8,128)(2,1)S(1)}, u32[]{:S(2)}, u32[]{:S(2)}) %collective-permute-start) | collective-permute-done | bytes 344096
  217.0 4.8 %concatenate = bf16[66,7168]{1,0:T(8,128)(2,1)S(1)} concatenate(bf16[18,7168]{1,0:T(8,128)(2,1)S(1)} %collective-permute-done.1, bf16[24,7168]{1,0:T(8,128)(2,1)S(1)} %collective-permute-done, bf16[24,7168]{1,0:T(8,128)(2,1)S(1)} %fusion), dimensions={0} | concatenate | bytes 1892352
  221.9 0.1 dynamic-slice_bitcast_fusion
  222.0 6.0 %copy.42 = bf16[1,18,7168]{1,0,2:T(2,128)(2,1)} copy(bf16[1,18,7168]{2,1,0:T(8,128)(2,1)S(1)} %dynamic-slice_bitcast_fusion) | data formatting | bytes 516096 | tf_op jit(solution)/shard_map/reduce_scatter | solution.py:33
  228.0 0.5 broadcast.68
  228.5 39.8 %reduce.4 = bf16[7168,18]{1,0:T(8,128)(2,1)S(1)} reduce(bf16[7168,1,18]{2,1,0:T(2,128)(2,1)} %bitcast.64, bf16[]{:T(256)} %broadcast.68), dimensions={1}, to_apply=%bitcast.56.reduce_sub_computation | reduce | bytes 516098
  268.3 3.4 reshape.114
  271.7 9.8 %all_to_all.34 = bf16[4,2,16128]{2,1,0:T(2,128)(2,1)S(1)} all-to-all(bf16[4,2,16128]{2,1,0:T(2,128)(2,1)S(1)} %reshape.114), channel_id=1, replica_groups=mesh['pipe'=4,'vocab'=2,'expert'=4] {'expert'}, dimensions={0} | all-to-all | bytes 516096 | tf_op jit(solution)/shard_map/all_to_all | solution.py:36
  281.4 5.2 %reshape.115 = bf16[7168,1,18]{2,1,0:T(2,128)(2,1)} reshape(bf16[4,2,16128]{2,1,0:T(2,128)(2,1)S(1)} %all_to_all.34) | data formatting | bytes 516096
  286.6 7.3 %copy.43 = bf16[1,18,7168]{2,1,0:T(8,128)(2,1)S(1)} copy(bf16[1,18,7168]{1,0,2:T(2,128)(2,1)} %bitcast.65) | data formatting | bytes 516096 | tf_op jit(solution)/shard_map/all_to_all | solution.py:36
  293.9 0.8 all_to_all.28
  294.7 0.3 reduce-scatter.5.cloned.1.call-start
  295.0 0.1 copy.46
  295.1 29.7 %all-gather.3.cloned.1.call-done = bf16[4,1,144,1792]{3,0,1,2:T(4,128)(2,1)} async-done(((bf16[4,1,18,1792]{3,0,1,2:T(4,128)(2,1)}), bf16[4,1,144,1792]{3,0,1,2:T(4,128)(2,1)}) %all-gather.3.cloned.1.call-update) | async-done | bytes 2064400 | tf_op jit(solution)/shard_map/all_gather | solution.py:39
  324.8 1.8 copy.45
  326.6 2.4 bitcast_convert_fusion
  329.0 6.1 %gather_fusion.1 = f32[384,1792]{1,0:T(8,128)S(1)} fusion(f32[576,1792]{1,0:T(8,128)} %bitcast_convert_fusion, s32[1024]{0:T(1024)S(1)} %pad_clamp_fusion), kind=kCustom, calls=%fused_computation.1 | custom fusion | bytes 5506560 | tf_op jit(solution)/shard_map/gather | solution.py:42
  335.1 2.8 reshape.75
  337.8 5.9 %multiply_reduce_fusion = f32[192,1792]{1,0:T(8,128)S(1)} fusion(f32[192,2,1792]{2,1,0:T(2,128)} %reshape.75, f32[192,2]{1,0:T(8,128)S(1)} %copy.46), kind=kLoop, calls=%fused_computation.11 | loop fusion | flops 1032192 | bytes 4130304 | tf_op jit(solution)/shard_map/reduce_sum | solution.py:45
  343.8 17.4 %convolution_convert_fusion = bf16[192,8192]{1,0:T(8,128)(2,1)} fusion(bf16[8192,1792]{1,0:T(8,128)(2,1)} %param.10, f32[192,1792]{1,0:T(8,128)S(1)} %multiply_reduce_fusion, bf16[192,1792]{1,0:T(8,128)(2,1)S(1)} %copy-done.1), kind=kOutput, calls=%fused_computation.3 | convolution fusion | flops 5639749632 | bytes 34570240 | tf_op jit(solution)/shard_map/dot_general | solution.py:48
  361.1 60.6 %reduce-scatter.5.cloned.1.call-done = bf16[48,8192]{1,0:T(8,128)(2,1)} async-done(((bf16[192,8192]{1,0:T(8,128)(2,1)}), bf16[48,8192]{1,0:T(8,128)(2,1)}) %reduce-scatter.5.cloned.1.call-update) | async-done | bytes 786448 | tf_op jit(solution)/shard_map/reduce_scatter | solution.py:47
  (21 shorter events, 0.2 us)
Async XLA Ops:
  6.5 75.1 %all-reduce.4.cloned.1.call-start = ((), (), s32[]{:S(2)}) async-start(), calls=%async_computation.3 | async-start | bytes 1376256 | tf_op jit(solution)/shard_map/psum | solution.py:18
  22.1 1.3 copy-start.2
  23.3 301.5 %all-gather.3.cloned.1.call-start = ((), (), s32[]{:S(2)}) async-start(), calls=%async_computation.5 | async-start | bytes 2322432 | tf_op jit(solution)/shard_map/all_gather | solution.py:39
  139.5 2.0 copy-start
  149.2 62.1 %copy-start.4 = (u32[32]{0:T(128)S(1)}, u32[32]{0:T(128)}, u32[]{:S(2)}) copy-start(u32[32]{0:T(128)} %constant.54) | copy-start | bytes 388
  207.6 9.5 %collective-permute-start = (bf16[24,7168]{1,0:T(8,128)(2,1)S(1)}, bf16[24,7168]{1,0:T(8,128)(2,1)S(1)}, u32[]{:S(2)}, u32[]{:S(2)}) collective-permute-start(bf16[24,7168]{1,0:T(8,128)(2,1)S(1)} %fusion), channel_id=1, source_target_pairs={{0,4},{4,8},{8,12},{12,16},{16,20},{20,24},{24,28},{1,5},{5,9},{9,... | collective-permute-start | bytes 1032200
  209.6 3.0 collective-permute-start.1
  286.6 8.4 %copy-start.3 = (f32[192,2]{0,1:T(2,128)S(1)}, f32[192,2]{0,1:T(2,128)}, u32[]{:S(2)}) copy-start(f32[192,2]{0,1:T(2,128)} %param.9) | copy-start | bytes 4612
  294.7 127.0 %reduce-scatter.5.cloned.1.call-start = ((), (), s32[]{:S(2)}) async-start(), calls=%async_computation.4 | async-start | bytes 3932160 | tf_op jit(solution)/shard_map/reduce_scatter | solution.py:47
  337.8 5.9 %copy-start.1 = (bf16[192,1792]{1,0:T(8,128)(2,1)S(1)}, bf16[192,1792]{1,0:T(8,128)(2,1)}, u32[]{:S(2)}) copy-start(bf16[192,1792]{1,0:T(8,128)(2,1)} %all-reduce.4.cloned.1.call-done) | copy-start | bytes 2064388
Sparse Core Ops, SparseCore 0:
  23.5 58.1 all-reduce.3
  294.8 29.9 all-gather.2
  361.3 60.3 reduce-scatter.4
where the time goes:
time: 429 us; the launch traced here: 428 us
  waiting for transfers between devices  151 us (35%)
  blocking collectives  119 us (28%)
  local copies, waits for them, and re-layouts  64 us (15%)
  other arithmetic  51.5 us (12%)
  matrix products  25 us (6%)
  between operations  14 us (3%)
    reduce_scatter x1, waiting for transfers between devices, per_device(): lax.psum_scatter(lax.dot_general(residual, embed_table, (((1,), (1,)), ((...  60.6 us
    unnamed x1, blocking collectives  58.3 us
    psum x1, waiting for transfers between devices, per_device(): embedded = lax.psum(lookup_rows.astype(jnp.bfloat16), ('pipe', 'vocab'))  55.8 us
    all_to_all x1, blocking collectives, per_device(): lax.all_to_all(buffer, 'expert', split_axis=0, concat_axis=2, tiled=True)[0]  51.2 us
    unnamed x2, other arithmetic  39.8 us
    all_gather x1, waiting for transfers between devices, per_device(): lax.all_gather(shared.astype(jnp.bfloat16), ('pipe', 'vocab'), axis=1, ti...  29.7 us
    dot_general x1, matrix products, per_device(): lax.dot_general(residual, embed_table, (((1,), (1,)), ((), ())), preferre...  17.4 us
    unnamed x20, local copies, waits for them, and re-layouts  16.9 us
  transfers between devices with their start and end apart: 5, of which 4 were waited for; matrix products, arithmetic and copies ran while one was open for 1% of the time, Pallas kernels for 0%

commit v1 on v0

--- a/solution.py
+++ b/solution.py
@@ -15,7 +15,8 @@
     in_shard = (local_ids >= 0) & (local_ids < vocab_rows)
     lookup_rows = jnp.take(embed_table, jnp.clip(local_ids, 0, vocab_rows - 1), axis=0)
     lookup_rows = jnp.where(in_shard[:, None], lookup_rows.astype(jnp.float32), 0.0)
-    embedded = lax.psum(lookup_rows.astype(jnp.bfloat16), ("pipe", "vocab"))
+    half = lax.psum(lookup_rows.astype(jnp.bfloat16), "vocab")
+    embedded = lax.psum(half, "pipe")
     flat_routes = routes.reshape(-1)
     one_hot = (flat_routes[:, None] == jnp.arange(experts, dtype=jnp.int32)[None, :]).astype(
         jnp.int32

time: 429 us -> 443 us (1.033)
  waiting for transfers between devices: 151 us -> 163 us
    psum x1 -> x2, waiting for transfers between devices: 55.8 us -> 69.1 us  [the longest x1 36.4 us: per_device(): embedded = lax.psum(half, 'pipe')]
  transfers between devices with their start and end apart: 5 -> 6, of which waited for: 4 -> 5; matrix products, arithmetic and copies ran while one was open for 1% -> 1% of each run, Pallas kernels for 0% -> 0%
where the time goes in v1:
time: 443 us; the launch traced here: 442 us
  waiting for transfers between devices  163 us (37%)
  blocking collectives  120 us (27%)
  local copies, waits for them, and re-layouts  64 us (14%)
  other arithmetic  51.5 us (12%)
  matrix products  25 us (6%)
  between operations  14 us (3%)
    reduce_scatter x1, waiting for transfers between devices, per_device(): lax.psum_scatter(lax.dot_general(residual, embed_table, (((1,), (1,)), ((...  60.6 us
    unnamed x1, blocking collectives  59.4 us
    all_to_all x1, blocking collectives, per_device(): lax.all_to_all(buffer, 'expert', split_axis=0, concat_axis=2, tiled=True)[0]  51 us
    unnamed x2, other arithmetic  39.8 us
    psum x1, waiting for transfers between devices, per_device(): embedded = lax.psum(half, 'pipe')  36.4 us
    psum x1, waiting for transfers between devices, per_device(): half = lax.psum(lookup_rows.astype(jnp.bfloat16), 'vocab')  32.7 us
    all_gather x1, waiting for transfers between devices, per_device(): lax.all_gather(shared.astype(jnp.bfloat16), ('pipe', 'vocab'), axis=1, ti...  29.3 us
    dot_general x1, matrix products, per_device(): lax.dot_general(residual, embed_table, (((1,), (1,)), ((), ())), preferre...  17.3 us
  transfers between devices with their start and end apart: 6, of which 5 were waited for; matrix products, arithmetic and copies ran while one was open for 1% of the time, Pallas kernels for 0%

profile of v1, /device:TPU:0, one launch (start us, length us, event | category | flops | bytes accessed | tf_op | source)
XLA Modules:
  0.0 442.1 jit_solution(10218511405683068279)
XLA Ops:
  6.5 0.7 compare_and_fusion
  7.2 14.9 %gather_fusion = bf16[192,1792]{1,0:T(8,128)(2,1)S(1)} fusion(bf16[8192,1792]{1,0:T(8,128)(2,1)} %param.10, s32[1024]{0:T(1024)S(1)} %pad_clamp_fusion.1), kind=kCustom, calls=%fused_computation | custom fusion | bytes 1377024 | tf_op jit(solution)/shard_map/jit(_take)/gather | solution.py:16
  22.1 1.2 select_convert_fusion
  23.4 0.1 copy.39
  23.5 0.1 eq.29
  23.7 0.1 eq.25
  23.8 1.2 reduce-window.6
  25.1 0.2 slice_reduce_fusion
  25.3 0.2 reduce-window.9
  25.5 0.1 copy.38
  25.6 0.1 mul.44
  25.7 32.7 %all-reduce.5.cloned.1.call-done = bf16[192,1792]{1,0:T(8,128)(2,1)} async-done(((bf16[192,1792]{1,0:T(8,128)(2,1)}), bf16[192,1792]{1,0:T(8,128)(2,1)}) %all-reduce.5.cloned.1.call-update) | async-done | bytes 688144 | tf_op jit(solution)/shard_map/psum | solution.py:18
  58.6 36.4 %all-reduce.7.cloned.1.call-done = bf16[192,1792]{1,0:T(8,128)(2,1)} async-done(((bf16[192,1792]{1,0:T(8,128)(2,1)}), bf16[192,1792]{1,0:T(8,128)(2,1)}) %all-reduce.7.cloned.1.call-update) | async-done | bytes 688144 | tf_op jit(solution)/shard_map/psum | solution.py:19
  95.0 1.8 broadcast_in_dim.42
  96.8 0.6 reshape.98
  97.4 3.3 scatter_custom_fusion
  100.7 51.0 %all_to_all.33 = bf16[4,144,1792]{2,1,0:T(8,128)(2,1)S(1)} all-to-all(bf16[4,144,1792]{2,1,0:T(8,128)(2,1)S(1)} %bitcast.66), channel_id=1, replica_groups=mesh['pipe'=4,'vocab'=2,'expert'=4] {'expert'}, dimensions={0} | all-to-all | bytes 4128768 | tf_op jit(solution)/shard_map/all_to_all | solution.py:29
  151.7 1.1 copy.41
  152.8 0.3 copy.50
  153.0 1.8 copy-done
  154.8 0.8 fusion.5
  155.6 6.9 %fusion.1 = bf16[1,144,7168]{2,1,0:T(8,128)(2,1)} fusion(bf16[1,256,7168]{2,1,0:T(8,128)(2,1)} %param.13, bf16[144,7168]{1,0:T(8,128)(2,1)S(1)} %bitcast.63, bf16[1,7168,256]{2,1,0:T(8,128)(2,1)} %param.12, f32[144,256]{1,0:T(8,128)S(1)} %fusion.5), kind=kOutput, calls=%fused_computation.5 | convolution fusion | flops 1058217984 | bytes 11616256 | tf_op jit(solution)/shard_map/dot_general | solution.py:33
  162.5 59.4 %fusion = bf16[24,7168]{1,0:T(8,128)(2,1)S(1)} fusion(bf16[1,144,7168]{2,1,0:T(8,128)(2,1)} %fusion.1), kind=kCustom, calls=%all-reduce-scatter | all-reduce-scatter fusion | flops 1376257 | bytes 2408960
  221.9 1.3 collective-permute-start
  223.2 0.1 slice.13
  223.3 2.3 collective-permute-start.1
  225.6 0.6 dynamic-slice.4
  226.8 4.5 %collective-permute-done = bf16[24,7168]{1,0:T(8,128)(2,1)S(1)} collective-permute-done((bf16[24,7168]{1,0:T(8,128)(2,1)S(1)}, bf16[24,7168]{1,0:T(8,128)(2,1)S(1)}, u32[]{:S(2)}, u32[]{:S(2)}) %collective-permute-start) | collective-permute-done | bytes 344096
  231.3 4.8 %concatenate = bf16[66,7168]{1,0:T(8,128)(2,1)S(1)} concatenate(bf16[18,7168]{1,0:T(8,128)(2,1)S(1)} %collective-permute-done.1, bf16[24,7168]{1,0:T(8,128)(2,1)S(1)} %collective-permute-done, bf16[24,7168]{1,0:T(8,128)(2,1)S(1)} %fusion), dimensions={0} | concatenate | bytes 1892352
  236.1 0.1 dynamic-slice_bitcast_fusion
  236.2 6.0 %copy.42 = bf16[1,18,7168]{1,0,2:T(2,128)(2,1)} copy(bf16[1,18,7168]{2,1,0:T(8,128)(2,1)S(1)} %dynamic-slice_bitcast_fusion) | data formatting | bytes 516096 | tf_op jit(solution)/shard_map/reduce_scatter | solution.py:34
  242.3 0.5 broadcast.68
  242.8 39.8 %reduce.4 = bf16[7168,18]{1,0:T(8,128)(2,1)S(1)} reduce(bf16[7168,1,18]{2,1,0:T(2,128)(2,1)} %bitcast.64, bf16[]{:T(256)} %broadcast.68), dimensions={1}, to_apply=%bitcast.56.reduce_sub_computation | reduce | bytes 516098
  282.5 3.4 reshape.114
  285.9 9.8 %all_to_all.34 = bf16[4,2,16128]{2,1,0:T(2,128)(2,1)S(1)} all-to-all(bf16[4,2,16128]{2,1,0:T(2,128)(2,1)S(1)} %reshape.114), channel_id=1, replica_groups=mesh['pipe'=4,'vocab'=2,'expert'=4] {'expert'}, dimensions={0} | all-to-all | bytes 516096 | tf_op jit(solution)/shard_map/all_to_all | solution.py:37
  295.7 5.2 %reshape.115 = bf16[7168,1,18]{2,1,0:T(2,128)(2,1)} reshape(bf16[4,2,16128]{2,1,0:T(2,128)(2,1)S(1)} %all_to_all.34) | data formatting | bytes 516096
  300.8 7.3 %copy.43 = bf16[1,18,7168]{2,1,0:T(8,128)(2,1)S(1)} copy(bf16[1,18,7168]{1,0,2:T(2,128)(2,1)} %bitcast.65) | data formatting | bytes 516096 | tf_op jit(solution)/shard_map/all_to_all | solution.py:37
  308.1 0.8 all_to_all.28
  309.0 0.3 reduce-scatter.5.cloned.1.call-start
  309.2 0.1 copy.46
  309.4 29.3 %all-gather.3.cloned.1.call-done = bf16[4,1,144,1792]{3,0,1,2:T(4,128)(2,1)} async-done(((bf16[4,1,18,1792]{3,0,1,2:T(4,128)(2,1)}), bf16[4,1,144,1792]{3,0,1,2:T(4,128)(2,1)}) %all-gather.3.cloned.1.call-update) | async-done | bytes 2064400 | tf_op jit(solution)/shard_map/all_gather | solution.py:40
  338.7 1.8 copy.45
  340.5 2.4 bitcast_convert_fusion
  342.8 6.1 %gather_fusion.1 = f32[384,1792]{1,0:T(8,128)S(1)} fusion(f32[576,1792]{1,0:T(8,128)} %bitcast_convert_fusion, s32[1024]{0:T(1024)S(1)} %pad_clamp_fusion), kind=kCustom, calls=%fused_computation.1 | custom fusion | bytes 5506560 | tf_op jit(solution)/shard_map/gather | solution.py:43
  348.9 2.8 reshape.75
  351.7 5.9 %multiply_reduce_fusion = f32[192,1792]{1,0:T(8,128)S(1)} fusion(f32[192,2,1792]{2,1,0:T(2,128)} %reshape.75, f32[192,2]{1,0:T(8,128)S(1)} %copy.46), kind=kLoop, calls=%fused_computation.11 | loop fusion | flops 1032192 | bytes 4130304 | tf_op jit(solution)/shard_map/reduce_sum | solution.py:46
  357.6 17.3 %convolution_convert_fusion = bf16[192,8192]{1,0:T(8,128)(2,1)} fusion(bf16[8192,1792]{1,0:T(8,128)(2,1)} %param.10, f32[192,1792]{1,0:T(8,128)S(1)} %multiply_reduce_fusion, bf16[192,1792]{1,0:T(8,128)(2,1)S(1)} %copy-done.1), kind=kOutput, calls=%fused_computation.3 | convolution fusion | flops 5639749632 | bytes 34570240 | tf_op jit(solution)/shard_map/dot_general | solution.py:49
  375.0 60.6 %reduce-scatter.5.cloned.1.call-done = bf16[48,8192]{1,0:T(8,128)(2,1)} async-done(((bf16[192,8192]{1,0:T(8,128)(2,1)}), bf16[48,8192]{1,0:T(8,128)(2,1)}) %reduce-scatter.5.cloned.1.call-update) | async-done | bytes 786448 | tf_op jit(solution)/shard_map/reduce_scatter | solution.py:48
  (24 shorter events, 0.3 us)
Async XLA Ops:
  6.5 51.9 %all-reduce.5.cloned.1.call-start = ((), (), s32[]{:S(2)}) async-start(), calls=%async_computation.3 | async-start | bytes 1376256 | tf_op jit(solution)/shard_map/psum | solution.py:18
  22.1 1.3 copy-start.2
  23.3 71.6 %all-reduce.7.cloned.1.call-start = ((), (), s32[]{:S(2)}) async-start(), calls=%async_computation.4 | async-start | bytes 1376256 | tf_op jit(solution)/shard_map/psum | solution.py:19
  58.5 280.2 %all-gather.3.cloned.1.call-start = ((), (), s32[]{:S(2)}) async-start(), calls=%async_computation.6 | async-start | bytes 2322432 | tf_op jit(solution)/shard_map/all_gather | solution.py:40
  152.8 2.0 copy-start
  162.5 63.1 %copy-start.4 = (u32[32]{0:T(128)S(1)}, u32[32]{0:T(128)}, u32[]{:S(2)}) copy-start(u32[32]{0:T(128)} %constant.54) | copy-start | bytes 388
  221.9 9.4 %collective-permute-start = (bf16[24,7168]{1,0:T(8,128)(2,1)S(1)}, bf16[24,7168]{1,0:T(8,128)(2,1)S(1)}, u32[]{:S(2)}, u32[]{:S(2)}) collective-permute-start(bf16[24,7168]{1,0:T(8,128)(2,1)S(1)} %fusion), channel_id=1, source_target_pairs={{0,4},{4,8},{8,12},{12,16},{16,20},{20,24},{24,28},{1,5},{5,9},{9,... | collective-permute-start | bytes 1032200
  223.3 3.5 collective-permute-start.1
  300.8 8.4 %copy-start.3 = (f32[192,2]{0,1:T(2,128)S(1)}, f32[192,2]{0,1:T(2,128)}, u32[]{:S(2)}) copy-start(f32[192,2]{0,1:T(2,128)} %param.9) | copy-start | bytes 4612
  309.0 126.6 %reduce-scatter.5.cloned.1.call-start = ((), (), s32[]{:S(2)}) async-start(), calls=%async_computation.5 | async-start | bytes 3932160 | tf_op jit(solution)/shard_map/reduce_scatter | solution.py:48
  351.7 5.9 %copy-start.1 = (bf16[192,1792]{1,0:T(8,128)(2,1)S(1)}, bf16[192,1792]{1,0:T(8,128)(2,1)}, u32[]{:S(2)}) copy-start(bf16[192,1792]{1,0:T(8,128)(2,1)} %all-reduce.7.cloned.1.call-done) | copy-start | bytes 2064388
Sparse Core Ops, SparseCore 0:
  23.5 34.9 all-reduce.4
  60.8 34.1 all-reduce.6
  309.1 29.5 all-gather.2
  375.1 60.3 reduce-scatter.4
